TPU v7x, 32 devices: a whole 2x2x4 slice. The times are simulated.
32 devices in a mesh: tm: 2 (over core), stn: 4 (over z), chan: 4 (over y, x).
Axes of the slice: x: 2, y: 2, z: 4, core: 2. Of those that a mesh axis runs over, the one named last changes fastest.
Arguments:
- voltages: bfloat16 [2, 8, 512, 32, 2, 256], P(None, 'chan', 'stn', 'tm'), may hold values from -100 to 100
- fir_taps: float32 [16, 256], replicated, may hold values from -1.5 to 1.5
- station_map: int32 [512], P('stn'), may hold values from 0 to 31, as said below
- beam_index: int32 [512], P('stn'), may hold values from 0 to 15
- weight_table: bfloat16 [2, 16, 8, 8], P(None, None, 'chan'), may hold values from -1.5 to 1.5
Outputs:
- visibilities: float32 [2, 2, 8, 32, 32, 8, 2, 2, 256], P('tm', None, 'chan', 'stn')
Inputs may be any that keep to these rules, and one draw needn't show every extreme that they name: `station_map`: each station number names exactly 16 dishes; of the dishes g * 128 up to (g + 1) * 128 - 1, exactly 32 name a station of the block h * 8 up to (h + 1) * 8 - 1, for every g and h.
All inputs are finite; a program needn't handle non-finite values.
Results may differ from a plain program's by a relative error of at most 0.017.
Values may be sent and summed in bfloat16 or wider, within the bound.
A program may use at most 512 MiB of HBM per device.

v0:
```python
import jax
import jax.numpy as jnp
from jax import lax
from jax.sharding import PartitionSpec as P

STATIONS = 32
COARSE = 8
epsilon = 1e-06


def shifted(value, axis, steps):
    count = lax.axis_size(axis)
    first, last = (max(0, -steps), min(count, count - steps))
    return lax.ppermute(value, axis, [(source, source + steps) for source in range(first, last)])


def dft_tables(length):
    bin_index = jnp.arange(length, dtype=jnp.int32)
    phase_step = bin_index[:, None] * bin_index[None, :] % length
    angles = phase_step.astype(jnp.float32) * (2.0 * jnp.pi / length)
    return (jnp.cos(angles).astype(jnp.bfloat16), jnp.sin(angles).astype(jnp.bfloat16))


def power_terms(formed):
    values = formed.astype(jnp.float32)
    return jnp.sum(values * values, axis=(1, 3, 4, 6))


def normalise(formed, power_sum, denominator):
    inverse_rms = lax.rsqrt(power_sum / denominator + epsilon)
    return (formed.astype(jnp.float32) * inverse_rms[:, None, :, None, None, :, None]).astype(
        jnp.bfloat16
    )


def correlate(left_beams, right_beams, frames_dev):

    def product(first_part, second_part):
        return jnp.einsum(
            "sbcfpk,tbcfqk->cstbpqk", first_part, second_part, preferred_element_type=jnp.float32
        )

    left_re = left_beams[:, 0]
    left_im = left_beams[:, 1]
    right_re = right_beams[:, 0]
    right_im = right_beams[:, 1]
    vis_re = product(left_re, right_re) + product(left_im, right_im)
    vis_im = product(left_im, right_re) - product(left_re, right_im)
    return jnp.stack([vis_re, vis_im]) / frames_dev


def mixing_of(row_hot, weight_table):
    weights = jnp.einsum("dt,otcb->ocdb", row_hot, weight_table, preferred_element_type=jnp.float32)
    weight_re = weights[0]
    weight_im = weights[1]
    return jnp.stack([jnp.stack([weight_re, -weight_im]), jnp.stack([weight_im, weight_re])])


def per_device(voltages, fir_taps, station_map, beam_index, weight_table):
    components, coarse_dev, dishes_dev, frames_dev, polars, fine_bins = voltages.shape
    history = fir_taps.shape[0] - 1
    table_rows = weight_table.shape[1]
    cosine, sine_table = dft_tables(fine_bins)
    earlier = shifted(voltages[:, :, :, frames_dev - history :], "tm", 1)
    extended = jnp.concatenate([earlier, voltages], axis=3)
    filtered = jnp.zeros(voltages.shape, jnp.float32)
    for tap_index in range(history + 1):
        offset = history - tap_index
        filtered = filtered + fir_taps[tap_index] * extended[
            :, :, :, offset : offset + frames_dev
        ].astype(jnp.float32)
    filtered = filtered.astype(jnp.bfloat16)
    real_part = filtered[0].reshape(-1, fine_bins)
    imag_part = filtered[1].reshape(-1, fine_bins)
    spec_re = jnp.dot(real_part, cosine, preferred_element_type=jnp.float32) + jnp.dot(
        imag_part, sine_table, preferred_element_type=jnp.float32
    )
    spec_im = jnp.dot(imag_part, cosine, preferred_element_type=jnp.float32) - jnp.dot(
        real_part, sine_table, preferred_element_type=jnp.float32
    )
    spectra = jnp.stack([spec_re, spec_im]).reshape(voltages.shape).astype(jnp.bfloat16)
    denominator = COARSE * frames_dev * fine_bins
    own_count = STATIONS // lax.axis_size("stn")
    station_hot = (station_map[:, None] == jnp.arange(STATIONS, dtype=jnp.int32)[None, :]).astype(
        jnp.float32
    )
    table_hot = (beam_index[:, None] == jnp.arange(table_rows, dtype=jnp.int32)[None, :]).astype(
        jnp.bfloat16
    )
    mixing = mixing_of(table_hot, weight_table)
    steering = (station_hot[None, None, None, :, :, None] * mixing[:, :, :, :, None, :]).astype(
        jnp.bfloat16
    )
    full_sums = jnp.einsum(
        "oicdsb,icdfpk->sobcfpk", steering, spectra, preferred_element_type=jnp.float32
    )
    formed = lax.psum(full_sums.astype(jnp.bfloat16), "stn")
    power_sum = lax.psum(power_terms(formed), "chan")
    normed = normalise(formed, power_sum, denominator)
    own_rows = lax.dynamic_slice_in_dim(normed, lax.axis_index("stn") * own_count, own_count, 0)
    visibility = correlate(own_rows, normed, frames_dev)
    return visibility[None]


def solution(mesh):
    in_specs = (
        P(None, "chan", "stn", "tm", None, None),
        P(),
        P("stn"),
        P("stn"),
        P(None, None, "chan", None),
    )
    out_specs = P("tm", None, "chan", "stn", None, None, None, None, None)
    return jax.shard_map(
        per_device, mesh=mesh, in_specs=in_specs, out_specs=out_specs, check_vma=False
    )
```

profile of v0, /device:TPU:0, one launch (start us, length us, event | category | flops | bytes accessed | tf_op | source)
XLA Modules:
  0.0 1312.8 jit_solution(9741827098668168143)
XLA Ops:
  6.5 0.0 copy-start
  6.5 0.0 all-reduce.2.cloned.1.call-start
  6.5 0.0 slice-start
  6.5 6.9 slice.122
  13.5 5.5 collective-permute-start
  18.9 0.0 copy-done
  18.9 0.8 fusion.20
  19.7 0.0 slice-start.1
  19.8 0.8 fusion.19
  20.6 1.1 fusion.40
  21.6 6.4 collective-permute-done
  28.0 6.8 constant_dynamic-update-slice_fusion.1
  34.8 0.0 slice-done
  34.8 0.0 slice-done.1
  34.8 8.4 constant_dynamic-update-slice_fusion
  43.3 108.3 %add_convert_fusion = bf16[2,2,128,16,2,256]{5,4,3,2,1,0:T(2,128)(2,1)} fusion(bf16[2,2,128,16,2,256]{5,4,3,2,1,0:T(2,128)(2,1)S(1)} %bitcast.86, bf16[2,2,128,31,2,256]{5,4,3,2,1,0:T(2,128)(2,1)S(1)} %constant_dynamic-update-slice_fusion, f32[256]{0:T(256)S(1)} %bitcast.102, f32[256]{0:T(256)S(1)} %bitcast.103, f32[256]{0:T(256)S(1)} %bitcast.89, ...), kind=kLoop, calls=%fused_computation.8 | loop fusion | flops 201326592 | bytes 142622720 | tf_op jit(solution)/shard_map/convert_element_type | solution.py:72
  151.6 10.2 fusion.39
  161.8 7.2 reshape_squeeze.6
  168.9 7.2 reshape_squeeze.7
  176.1 0.0 copy-start.3
  176.1 4.5 fusion.17
  180.6 0.0 copy-done.3
  180.6 5.6 fusion.18
  186.2 4.2 fusion.4
  190.4 7.3 stack.35
  197.8 0.0 copy-start.2
  197.8 7.7 copy.19
  205.5 0.0 copy-done.2
  205.5 6.4 fusion.3
  211.9 7.2 stack.34
  219.1 5.6 copy.18
  224.7 10.1 fusion.2
  234.8 0.0 all-reduce.2.cloned.1.call-update
  234.9 564.4 %all-reduce.2.cloned.1.call-done = bf16[32,2,8,2,16,2,256]{6,0,2,1,5,4,3:T(8,128)(2,1)} async-done(((bf16[32,2,8,2,16,2,256]{6,0,2,1,5,4,3:T(8,128)(2,1)}), bf16[32,2,8,2,16,2,256]{6,0,2,1,5,4,3:T(8,128)(2,1)}) %all-reduce.2.cloned.1.call-update) | async-done | bytes 16777232 | tf_op jit(solution)/shard_map/psum | solution.py:97
  799.3 7.4 fusion
  806.7 10.0 psum.15
  816.7 12.7 fusion.1
  829.4 6.4 slice_bitcast_fusion
  835.8 2.0 dynamic-slice_bitcast_fusion.1
  837.8 22.6 %copy.36 = bf16[8,8,2,16,2,256,1]{3,0,4,6,5,1,2:T(8,128)(2,1)} copy(bf16[8,8,2,16,2,256,1]{5,0,1,4,3,2,6:T(8,128)(2,1)} %get-tuple-element.5) | data formatting | bytes 4194304 | tf_op jit(solution)/shard_map/squeeze | solution.py:43
  860.4 16.6 %copy.38 = bf16[8,8,2,16,2,256,1]{3,0,4,6,5,1,2:T(8,128)(2,1)} copy(bf16[8,8,2,16,2,256,1]{5,0,1,4,3,2,6:T(8,128)(2,1)S(1)} %get-tuple-element.6) | data formatting | bytes 4194304 | tf_op jit(solution)/shard_map/squeeze | solution.py:44
  877.0 44.4 %copy.37 = bf16[32,8,2,16,2,256,1]{0,3,6,4,5,1,2:T(8,128)(2,1)} copy(bf16[32,8,2,16,2,256,1]{5,0,1,4,3,2,6:T(8,128)(2,1)} %get-tuple-element.7) | data formatting | bytes 16777216 | tf_op jit(solution)/shard_map/squeeze | solution.py:46
  921.4 44.4 %copy.35 = bf16[32,8,2,16,2,256,1]{0,3,6,4,5,1,2:T(8,128)(2,1)} copy(bf16[32,8,2,16,2,256,1]{5,0,1,4,3,2,6:T(8,128)(2,1)} %get-tuple-element.8) | data formatting | bytes 16777216 | tf_op jit(solution)/shard_map/squeeze | solution.py:45
  965.8 39.2 %fusion.42 = f32[2,8,256,32,2,8,2]{3,5,6,4,2,1,0:T(8,128)} fusion(bf16[32,8,2,16,2,256,1]{0,3,6,4,5,1,2:T(8,128)(2,1)} %copy.35, bf16[8,8,2,16,2,256,1]{3,0,4,6,5,1,2:T(8,128)(2,1)} %copy.38), kind=kOutput, calls=%fused_computation.70 | convolution fusion | flops 134217728 | bytes 27262976 | tf_op jit(solution)/shard_map/sbcfpk,tbcfqk->cstbpqk/dot_general | solution.py:39
  1005.0 39.2 %fusion.41 = f32[2,8,256,32,2,8,2]{3,5,6,4,2,1,0:T(8,128)} fusion(bf16[32,8,2,16,2,256,1]{0,3,6,4,5,1,2:T(8,128)(2,1)} %copy.35, bf16[8,8,2,16,2,256,1]{3,0,4,6,5,1,2:T(8,128)(2,1)} %copy.36), kind=kOutput, calls=%fused_computation.69 | convolution fusion | flops 134217728 | bytes 27262976 | tf_op jit(solution)/shard_map/sbcfpk,tbcfqk->cstbpqk/dot_general | solution.py:39
  1044.2 60.2 %subtract_bitcast_fusion = f32[1,1,2,8,32,8,2,2,256]{4,3,6,7,8,5,2,1,0:T(8,128)} fusion(f32[2,8,256,32,2,8,2]{3,5,6,4,2,1,0:T(8,128)} %fusion.42, bf16[32,8,2,16,2,256,1]{0,3,6,4,5,1,2:T(8,128)(2,1)} %copy.37, bf16[8,8,2,16,2,256,1]{3,0,4,6,5,1,2:T(8,128)(2,1)} %copy.36), kind=kOutput, calls=%fused_computation | convolution fusion | flops 138412032 | bytes 44040192 | tf_op jit(solution)/shard_map/sbcfpk,tbcfqk->cstbpqk/dot_general | solution.py:39
  1104.4 34.7 %copy.30 = f32[1,1,2,8,32,8,2,2,256]{8,5,7,6,4,3,2,1,0:T(8,128)} copy(f32[1,1,2,8,32,8,2,2,256]{4,3,6,7,8,5,2,1,0:T(8,128)} %subtract_bitcast_fusion) | data formatting | bytes 33554432 | tf_op jit(solution)/shard_map/stack | solution.py:49
  1139.1 60.5 %add_bitcast_fusion = f32[1,1,2,8,32,8,2,2,256]{4,3,6,7,8,5,2,1,0:T(8,128)} fusion(f32[2,8,256,32,2,8,2]{3,5,6,4,2,1,0:T(8,128)} %fusion.41, bf16[32,8,2,16,2,256,1]{0,3,6,4,5,1,2:T(8,128)(2,1)} %copy.37, bf16[8,8,2,16,2,256,1]{3,0,4,6,5,1,2:T(8,128)(2,1)} %copy.38), kind=kOutput, calls=%fused_computation.1 | convolution fusion | flops 138412032 | bytes 44040192 | tf_op jit(solution)/shard_map/sbcfpk,tbcfqk->cstbpqk/dot_general | solution.py:39
  1199.5 34.8 %copy.29 = f32[1,1,2,8,32,8,2,2,256]{8,5,7,6,4,3,2,1,0:T(8,128)} copy(f32[1,1,2,8,32,8,2,2,256]{4,3,6,7,8,5,2,1,0:T(8,128)} %add_bitcast_fusion) | data formatting | bytes 33554432 | tf_op jit(solution)/shard_map/stack | solution.py:49
  1234.3 24.9 %maximum_multiply_fusion = f32[1,2,2,8,32,8,2,2,256]{8,5,7,6,4,3,2,1,0:T(8,128)} fusion(f32[1,1,2,8,32,8,2,2,256]{8,5,7,6,4,3,2,1,0:T(8,128)} %copy.30, f32[1,1,2,8,32,8,2,2,256]{8,5,7,6,4,3,2,1,0:T(8,128)} %copy.29), kind=kLoop, calls=%fused_computation.6 | loop fusion | flops 16777216 | bytes 67108864 | tf_op jit(solution)/shard_map/div | solution.py:49
  1259.2 0.0 copy-start.1
  1259.2 46.3 %copy.31 = f32[1,2,2,8,32,8,2,2,256]{8,7,6,5,4,3,2,1,0:T(2,128)} copy(f32[1,2,2,8,32,8,2,2,256]{8,5,7,6,4,3,2,1,0:T(8,128)} %maximum_multiply_fusion) | data formatting | bytes 67108864 | tf_op jit(solution)/shard_map/div | solution.py:49
  1305.5 0.0 copy-done.1
  (6 shorter events, 0.0 us)
Async XLA Ops:
  6.5 12.4 copy-start
  6.5 792.8 %all-reduce.2.cloned.1.call-start = ((), (), s32[]{:S(2)}) async-start(), calls=%async_computation | async-start | bytes 33554432 | tf_op jit(solution)/shard_map/psum | solution.py:97
  6.5 28.2 %slice-start = ((s8[8388608]{0:T(1024)(128)(4,1)}), s8[4194304]{0:T(1024)(128)(4,1)S(1)}, s32[]{:S(2)}) async-start(s8[8388608]{0:T(1024)(128)(4,1)} %bitcast.85), calls=%async_computation.1 | async-start | bytes 8388608
  13.5 14.6 %collective-permute-start = (bf16[2,2,128,15,2,256]{5,4,3,2,1,0:T(2,128)(2,1)S(1)}, bf16[2,2,128,15,2,256]{5,4,3,2,1,0:T(2,128)(2,1)}, u32[]{:S(2)}, u32[]{:S(2)}) collective-permute-start(bf16[2,2,128,15,2,256]{5,4,3,2,1,0:T(2,128)(2,1)S(1)} %slice.122), channel_id=1, source_target_pairs={{0,16},{1,17},{2,18},{3,19},{4,20},{5,21},{6,22},{7,23},{8,24},{9,... | collective-permute-start | bytes 23592968 | tf_op jit(solution)/shard_map/ppermute | solution.py:14
  19.7 15.1 %slice-start.1 = ((s8[8388608]{0:T(1024)(128)(4,1)}), s8[4194304]{0:T(1024)(128)(4,1)S(1)}, s32[]{:S(2)}) async-start(s8[8388608]{0:T(1024)(128)(4,1)} %bitcast.85), calls=%async_computation.2 | async-start | bytes 8388608
  176.1 4.5 copy-start.3
  197.8 7.7 copy-start.2
  1259.2 46.3 %copy-start.1 = (bf16[2,16,2,8]{1,3,2,0:T(8,128)(2,1)S(1)}, bf16[2,16,2,8]{1,3,2,0:T(8,128)(2,1)}, u32[]{:S(2)}) copy-start(bf16[2,16,2,8]{1,3,2,0:T(8,128)(2,1)} %param.9) | copy-start | bytes 3076
Sparse Core Ops, SparseCore 0:
  235.0 564.2 all-reduce.1
where the time goes:
time: 1320 us; the launch traced here: 1310 us
  waiting for transfers between devices  571 us (43%)
  local copies, waits for them, and re-layouts  328 us (25%)
  matrix products  231 us (18%)
  other arithmetic  154 us (12%)
  between operations  14 us (1%)
    psum x1, waiting for transfers between devices, per_device(): formed = lax.psum(full_sums.astype(jnp.bfloat16), 'stn')  564 us
    dot_general x4, matrix products, product(): jnp.einsum('sbcfpk,tbcfqk->cstbpqk', first_part, second_part, preferred_e...  199 us
    convert_element_type x1, other arithmetic, per_device(): filtered = filtered.astype(jnp.bfloat16)  108 us
    another operation x2, local copies, waits for them, and re-layouts, correlate(): return jnp.stack([vis_re, vis_im]) / frames_dev  69.5 us
    squeeze x2, local copies, waits for them, and re-layouts, correlate(): right_im = right_beams[:, 1]  50.9 us
    div x1, local copies, waits for them, and re-layouts, correlate(): return jnp.stack([vis_re, vis_im]) / frames_dev  46.3 us
    squeeze x1, local copies, waits for them, and re-layouts, correlate(): right_re = right_beams[:, 0]  44.4 us
    another operation x4, local copies, waits for them, and re-layouts, per_device(): jnp.stack([spec_re, spec_im]).reshape(voltages.shape).astype(jnp.bfloat16)  27.9 us
  transfers between devices with their start and end apart: 2, of which 2 were waited for; matrix products, arithmetic and copies ran while one was open for 0% of the time, Pallas kernels for 0%

commit v1 on v0

--- a/solution.py
+++ b/solution.py
@@ -94,7 +94,9 @@
     full_sums = jnp.einsum(
         "oicdsb,icdfpk->sobcfpk", steering, spectra, preferred_element_type=jnp.float32
     )
-    formed = lax.psum(full_sums.astype(jnp.bfloat16), "stn")
+    block = full_sums.astype(jnp.bfloat16)
+    parts = lax.all_gather(block, "stn")
+    formed = jnp.sum(parts, axis=0)
     power_sum = lax.psum(power_terms(formed), "chan")
     normed = normalise(formed, power_sum, denominator)
     own_rows = lax.dynamic_slice_in_dim(normed, lax.axis_index("stn") * own_count, own_count, 0)

time: 1320 us -> 2280 us (1.73)
  waiting for transfers between devices: 571 us -> 1120 us
  matrix products: 231 us -> 416 us
  other arithmetic: 154 us -> 298 us
  local copies, waits for them, and re-layouts: 328 us -> 404 us
    all_gather x0 -> x1, waiting for transfers between devices: none -> 1110 us  [per_device(): parts = lax.all_gather(block, 'stn')]
    psum x1 -> x0, waiting for transfers between devices: 564 us -> none  [per_device(): formed = lax.psum(full_sums.astype(jnp.bfloat16), 'stn')]
    reduce_sum x0 -> x1, local copies, waits for them, and re-layouts: none -> 213 us  [per_device(): formed = jnp.sum(parts, axis=0)]
    dot_general x4, matrix products: 199 us -> 384 us  [product(): jnp.einsum('sbcfpk,tbcfqk->cstbpqk', first_part, second_part, preferred_e...]
    squeeze x6 -> x0, local copies, waits for them, and re-layouts: 136 us -> none  [the longest x2 50.9 us: correlate(): right_im = right_beams[:, 1]]
    convert_element_type x1, other arithmetic: 12.7 us -> 88.3 us  [normalise(): (formed.astype(jnp.float32) * inverse_rms[:, None, :, None, None, :, None...]
    reduce_sum x1, other arithmetic: 7.38 us -> 44.7 us  [power_terms(): return jnp.sum(values * values, axis=(1, 3, 4, 6))]
    reduce_sum x0 -> x1, other arithmetic: none -> 30.8 us  [per_device(): formed = jnp.sum(parts, axis=0)]
where the time goes in v1:
time: 2280 us; the launch traced here: 2270 us
  waiting for transfers between devices  1120 us (49%)
  matrix products  416 us (18%)
  local copies, waits for them, and re-layouts  404 us (18%)
  other arithmetic  298 us (13%)
    all_gather x1, waiting for transfers between devices, per_device(): parts = lax.all_gather(block, 'stn')  1110 us
    dot_general x4, matrix products, product(): jnp.einsum('sbcfpk,tbcfqk->cstbpqk', first_part, second_part, preferred_e...  384 us
    reduce_sum x1, local copies, waits for them, and re-layouts, per_device(): formed = jnp.sum(parts, axis=0)  213 us
    convert_element_type x1, other arithmetic, per_device(): filtered = filtered.astype(jnp.bfloat16)  108 us
    convert_element_type x1, other arithmetic, normalise(): (formed.astype(jnp.float32) * inverse_rms[:, None, :, None, None, :, None...  88.3 us
    another operation x2, local copies, waits for them, and re-layouts, correlate(): return jnp.stack([vis_re, vis_im]) / frames_dev  69.4 us
    div x1, local copies, waits for them, and re-layouts, correlate(): return jnp.stack([vis_re, vis_im]) / frames_dev  46.3 us
  transfers between devices with their start and end apart: 2, of which 2 were waited for; matrix products, arithmetic and copies ran while one was open for 0% of the time, Pallas kernels for 0%

profile of v1, /device:TPU:0, one launch (start us, length us, event | category | flops | bytes accessed | tf_op | source)
XLA Modules:
  0.0 2266.2 jit_solution(7291640760725465447)
XLA Ops:
  6.5 0.0 copy-start
  6.5 0.0 all-gather.3.cloned.1.call-start
  6.5 0.0 slice-start
  6.5 6.9 slice.122
  13.5 5.5 collective-permute-start
  18.9 0.0 copy-done
  18.9 0.8 fusion.24
  19.7 0.0 slice-start.1
  19.8 0.8 fusion.23
  20.6 1.1 fusion.48
  21.7 6.3 collective-permute-done
  28.0 6.8 constant_dynamic-update-slice_fusion.1
  34.8 0.0 slice-done
  34.8 0.0 slice-done.1
  34.8 8.4 constant_dynamic-update-slice_fusion
  43.3 108.3 %add_convert_fusion = bf16[2,2,128,16,2,256]{5,4,3,2,1,0:T(2,128)(2,1)} fusion(bf16[2,2,128,16,2,256]{5,4,3,2,1,0:T(2,128)(2,1)S(1)} %bitcast.123, bf16[2,2,128,31,2,256]{5,4,3,2,1,0:T(2,128)(2,1)S(1)} %constant_dynamic-update-slice_fusion, f32[256]{0:T(256)S(1)} %bitcast.139, f32[256]{0:T(256)S(1)} %bitcast.140, f32[256]{0:T(256)S(1)} %bitcast.126, ...), kind=kLoop, calls=%fused_computation.16 | loop fusion | flops 201326592 | bytes 142622720 | tf_op jit(solution)/shard_map/convert_element_type | solution.py:72
  151.6 10.2 fusion.47
  161.7 7.2 reshape_squeeze.6
  168.9 7.2 reshape_squeeze.7
  176.1 0.0 copy-start.3
  176.1 4.5 fusion.21
  180.6 0.0 copy-done.3
  180.6 5.6 fusion.22
  186.2 4.2 fusion.8
  190.4 7.4 stack.35
  197.8 0.0 copy-start.2
  197.8 7.8 copy.15
  205.5 0.0 copy-done.2
  205.5 6.4 fusion.7
  211.9 7.2 stack.34
  219.1 5.6 copy.14
  224.7 10.3 fusion.6
  235.1 0.0 all-gather.3.cloned.1.call-update
  235.1 1112.8 %all-gather.3.cloned.1.call-done = bf16[128,2,8,2,16,2,256]{6,0,2,1,5,4,3:T(8,128)(2,1)} async-done(((bf16[32,2,8,2,16,2,256]{6,0,2,1,5,4,3:T(8,128)(2,1)}), bf16[128,2,8,2,16,2,256]{6,0,2,1,5,4,3:T(8,128)(2,1)}) %all-gather.3.cloned.1.call-update) | async-done | bytes 67108880 | tf_op jit(solution)/shard_map/all_gather | solution.py:98
  1347.9 30.8 %reduce_sum.21 = bf16[32,2,8,2,16,2,256]{6,0,2,1,5,4,3:T(8,128)(2,1)} reduce(bf16[4,32,2,8,2,16,2,256]{7,1,0,3,2,6,5,4:T(8,128)(2,1)} %bitcast.30, bf16[]{:T(256)} %constant.30.clone.1), dimensions={0}, to_apply=%region_0.1 | reduce | flops 25165824 | bytes 83886080 | tf_op jit(solution)/shard_map/reduce_sum | solution.py:99
  1378.7 212.6 %copy.17 = bf16[32,2,8,2,16,2,256]{4,0,5,6,2,3,1:T(8,128)(2,1)} copy(bf16[32,2,8,2,16,2,256]{6,0,2,1,5,4,3:T(8,128)(2,1)} %reduce_sum.21) | data formatting | bytes 33554432 | tf_op jit(solution)/shard_map/reduce_sum | solution.py:99
  1591.3 44.7 %fusion = f32[32,8,2]{0,2,1:T(2,128)S(1)} fusion(bf16[32,2,8,2,16,2,256]{4,0,5,6,2,3,1:T(8,128)(2,1)} %copy.17), kind=kLoop, calls=%fused_computation.2 | loop fusion | flops 25165312 | bytes 16779264 | tf_op jit(solution)/shard_map/reduce_sum | solution.py:26
  1636.1 10.0 psum.7
  1646.1 88.3 %fusion.1 = bf16[32,2,8,2,16,2,256]{4,0,5,6,2,3,1:T(8,128)(2,1)} fusion(bf16[32,2,8,2,16,2,256]{4,0,5,6,2,3,1:T(8,128)(2,1)} %copy.17, f32[32,8,2]{0,2,1:T(2,128)S(1)} %add_rsqrt_fusion), kind=kLoop, calls=%fused_computation.3 | loop fusion | flops 25165824 | bytes 33556480 | tf_op jit(solution)/shard_map/convert_element_type | solution.py:31
  1734.4 94.8 %fusion.3 = f32[2,8,256,32,2,8,2]{3,5,6,4,2,1,0:T(8,128)} fusion(bf16[32,2,8,2,16,2,256]{4,0,5,6,2,3,1:T(8,128)(2,1)} %fusion.1, s32[]{:T(128)S(6)} %select_n.17), kind=kOutput, calls=%fused_computation.9 | convolution fusion | flops 134217728 | bytes 100663296 | tf_op jit(solution)/shard_map/sbcfpk,tbcfqk->cstbpqk/dot_general | solution.py:39
  1829.1 94.8 %fusion.2 = f32[2,8,256,32,2,8,2]{3,5,6,4,2,1,0:T(8,128)} fusion(bf16[32,2,8,2,16,2,256]{4,0,5,6,2,3,1:T(8,128)(2,1)} %fusion.1, s32[]{:T(128)S(6)} %select_n.17, s32[]{:T(128)S(6)} %add.99), kind=kOutput, calls=%fused_computation.8 | convolution fusion | flops 134217728 | bytes 100663304 | tf_op jit(solution)/shard_map/sbcfpk,tbcfqk->cstbpqk/dot_general | solution.py:39
  1923.9 97.4 %subtract_bitcast_fusion = f32[1,1,2,8,32,8,2,2,256]{4,3,6,7,8,5,2,1,0:T(8,128)} fusion(f32[2,8,256,32,2,8,2]{3,5,6,4,2,1,0:T(8,128)} %fusion.2, bf16[32,2,8,2,16,2,256]{4,0,5,6,2,3,1:T(8,128)(2,1)} %fusion.1, s32[]{:T(128)S(6)} %select_n.17), kind=kOutput, calls=%fused_computation.6 | convolution fusion | flops 138412032 | bytes 167772160 | tf_op jit(solution)/shard_map/sbcfpk,tbcfqk->cstbpqk/dot_general | solution.py:39
  2021.3 34.7 %copy.23 = f32[1,1,2,8,32,8,2,2,256]{8,5,7,6,4,3,2,1,0:T(8,128)} copy(f32[1,1,2,8,32,8,2,2,256]{4,3,6,7,8,5,2,1,0:T(8,128)} %subtract_bitcast_fusion) | data formatting | bytes 33554432 | tf_op jit(solution)/shard_map/stack | solution.py:49
  2056.0 97.2 %add_bitcast_fusion = f32[1,1,2,8,32,8,2,2,256]{4,3,6,7,8,5,2,1,0:T(8,128)} fusion(f32[2,8,256,32,2,8,2]{3,5,6,4,2,1,0:T(8,128)} %fusion.3, bf16[32,2,8,2,16,2,256]{4,0,5,6,2,3,1:T(8,128)(2,1)} %fusion.1, s32[]{:T(128)S(6)} %select_n.17, s32[]{:T(128)S(6)} %add.99), kind=kOutput, calls=%fused_computation.7 | convolution fusion | flops 138412032 | bytes 167772160 | tf_op jit(solution)/shard_map/sbcfpk,tbcfqk->cstbpqk/dot_general | solution.py:39
  2153.2 34.8 %copy.22 = f32[1,1,2,8,32,8,2,2,256]{8,5,7,6,4,3,2,1,0:T(8,128)} copy(f32[1,1,2,8,32,8,2,2,256]{4,3,6,7,8,5,2,1,0:T(8,128)} %add_bitcast_fusion) | data formatting | bytes 33554432 | tf_op jit(solution)/shard_map/stack | solution.py:49
  2188.0 24.9 %maximum_multiply_fusion = f32[1,2,2,8,32,8,2,2,256]{8,5,7,6,4,3,2,1,0:T(8,128)} fusion(f32[1,1,2,8,32,8,2,2,256]{8,5,7,6,4,3,2,1,0:T(8,128)} %copy.23, f32[1,1,2,8,32,8,2,2,256]{8,5,7,6,4,3,2,1,0:T(8,128)} %copy.22), kind=kLoop, calls=%fused_computation.12 | loop fusion | flops 16777216 | bytes 67108864 | tf_op jit(solution)/shard_map/div | solution.py:49
  2212.9 0.0 copy-start.1
  2212.9 46.3 %copy.24 = f32[1,2,2,8,32,8,2,2,256]{8,7,6,5,4,3,2,1,0:T(2,128)} copy(f32[1,2,2,8,32,8,2,2,256]{8,5,7,6,4,3,2,1,0:T(8,128)} %maximum_multiply_fusion) | data formatting | bytes 67108864 | tf_op jit(solution)/shard_map/div | solution.py:49
  2259.2 0.0 copy-done.1
  (6 shorter events, 0.0 us)
Async XLA Ops:
  6.5 12.4 copy-start
  6.5 1341.4 %all-gather.3.cloned.1.call-start = ((), (), s32[]{:S(2)}) async-start(), calls=%async_computation | async-start | bytes 83886080 | tf_op jit(solution)/shard_map/all_gather | solution.py:98
  6.5 28.2 %slice-start = ((s8[8388608]{0:T(1024)(128)(4,1)}), s8[4194304]{0:T(1024)(128)(4,1)S(1)}, s32[]{:S(2)}) async-start(s8[8388608]{0:T(1024)(128)(4,1)} %bitcast.122), calls=%async_computation.1 | async-start | bytes 8388608
  13.5 14.6 collective-permute-start
  19.7 15.1 slice-start.1
  176.1 4.5 copy-start.3
  197.8 7.8 copy-start.2
  2212.9 46.3 %copy-start.1 = (bf16[2,16,2,8]{1,3,2,0:T(8,128)(2,1)S(1)}, bf16[2,16,2,8]{1,3,2,0:T(8,128)(2,1)}, u32[]{:S(2)}) copy-start(bf16[2,16,2,8]{1,3,2,0:T(8,128)(2,1)} %param.9) | copy-start | bytes 3076
Sparse Core Ops, SparseCore 0:
  235.2 1112.6 all-gather.2
